TPU v7x, 32 devices: a whole 2x2x4 slice. The times are simulated.
32 devices in a mesh: row: 4 (over y, x), col: 8 (over z, core).
Axes of the slice: x: 2, y: 2, z: 4, core: 2. Of those that a mesh axis runs over, the one named last changes fastest.
Arguments:
- residuals: bfloat16 [32768, 768], P(('row', 'col')), may hold values from -6 to 6
- codes: int32 [32768, 64], P(('row', 'col')), may hold values from 0 to 255
- list_ids: int32 [32768], P(('row', 'col')), may hold values from 0 to 8191, as said below
- rotation: bfloat16 [768, 768], replicated, may hold values from -0.21875 to 0.21875
- codebook: bfloat16 [256, 768], replicated, may hold values from -6 to 6
- list_fill: int32 [8192], P(('row', 'col')), may hold values from 0 to 4095
Outputs:
- list_drift: float32 [8192, 768], P(('row', 'col'))
- list_counts: int32 [8192], P(('row', 'col'))
- new_blocks: int32 [8192], P(('row', 'col'))
Inputs may be any that keep to these rules, and one draw needn't show every extreme that they name: `list_ids`: lists are grouped in blocks of 256 consecutive ids. Among the rows of one device (aligned blocks of 1024 rows), at most 96 have lists in the same block, and in every such aligned block some list block is named by exactly 96 rows.
All inputs are finite; a program needn't handle non-finite values.
Results may differ from a plain program's by a relative error of at most 0.0029.
Values may be sent and summed in bfloat16 or wider, within the bound.
No kernel may reach another device: no remote copies, remote signals or barrier semaphores. Data moves between devices by JAX's collectives and lax.ppermute only.
A program may use at most 64 MiB of HBM per device.

v0:
```python
import jax
import jax.numpy as jnp
from jax import lax
from jax.sharding import PartitionSpec as P


def decode_rows(codes, codebook):
    vec_rows, sub_count = codes.shape
    cent_count, feat_width = codebook.shape
    sub_width = feat_width // sub_count
    code_table = codebook.reshape(cent_count, sub_count, sub_width)
    block_rows = 256
    code_blocks = codes.reshape(vec_rows // block_rows, block_rows, sub_count)

    def one_block(code_block):
        picker = (
            code_block[:, :, None] == jnp.arange(cent_count, dtype=jnp.int32)[None, None, :]
        ).astype(jnp.bfloat16)
        picked = jnp.einsum("bmk,kmj->bmj", picker, code_table, preferred_element_type=jnp.float32)
        return picked.reshape(block_rows, feat_width)

    return lax.map(one_block, code_blocks).reshape(vec_rows, feat_width)


def sum_by_list(rows_in, tags_in, list_total):
    picker = (tags_in[:, None] == jnp.arange(list_total, dtype=jnp.int32)[None, :]).astype(
        jnp.bfloat16
    )
    list_sums = lax.dot_general(
        picker, rows_in, (((0,), (0,)), ((), ())), preferred_element_type=jnp.float32
    )
    counts = jnp.sum(picker, axis=0, dtype=jnp.float32)
    return (list_sums, counts)


def rank_in_block(owner_block, owner_total):
    vec_rows = owner_block.shape[0]
    picker = (owner_block[:, None] == jnp.arange(owner_total, dtype=jnp.int32)[None, :]).astype(
        jnp.bfloat16
    )
    later = (
        jnp.arange(vec_rows, dtype=jnp.int32)[:, None]
        > jnp.arange(vec_rows, dtype=jnp.int32)[None, :]
    )
    before = jnp.dot(later.astype(jnp.bfloat16), picker, preferred_element_type=jnp.float32)
    return jnp.sum(before * picker.astype(jnp.float32), axis=1).astype(jnp.int32)


def local(residuals, codes, list_ids, rotation, codebook, list_fill):
    row_count = lax.axis_size("row")
    col_count = lax.axis_size("col")
    owner_total = row_count * col_count
    vec_rows, feat_width = residuals.shape
    lists_here = list_fill.shape[0]
    slot_cap = 3 * vec_rows // owner_total
    rotated = jnp.dot(residuals, rotation, preferred_element_type=jnp.float32)
    rebuilt = decode_rows(codes, codebook)
    encode_error = (rotated - rebuilt).astype(jnp.bfloat16)
    owner_block = list_ids // lists_here
    slot_index = owner_block * slot_cap + rank_in_block(owner_block, owner_total)
    send_rows = (
        jnp.zeros((owner_total * slot_cap, feat_width), jnp.bfloat16)
        .at[slot_index]
        .set(encode_error)
    )
    send_tags = jnp.full((owner_total * slot_cap,), -1, jnp.int32).at[slot_index].set(list_ids)
    send_rows = send_rows.reshape(row_count, col_count, slot_cap, feat_width)
    send_tags = send_tags.reshape(row_count, col_count, slot_cap)
    got_rows, got_tags = (
        lax.all_to_all(
            lax.all_to_all(send_rows, "row", split_axis=0, concat_axis=0, tiled=True),
            "col",
            split_axis=1,
            concat_axis=1,
            tiled=True,
        ),
        lax.all_to_all(
            lax.all_to_all(send_tags, "row", split_axis=0, concat_axis=0, tiled=True),
            "col",
            split_axis=1,
            concat_axis=1,
            tiled=True,
        ),
    )
    got_rows = got_rows.reshape(-1, feat_width)
    got_tags = got_tags.reshape(-1)
    list_base = (lax.axis_index("row") * col_count + lax.axis_index("col")) * lists_here
    local_index = jnp.where(got_tags >= 0, got_tags - list_base, -1)
    list_sums, counts = sum_by_list(got_rows, local_index, lists_here)
    list_counts = counts.astype(jnp.int32)
    divisor = jnp.maximum(list_counts, 1).astype(jnp.float32)
    list_drift = list_sums / divisor[:, None]
    new_blocks = (list_fill + list_counts + 127) // 128 - (list_fill + 127) // 128
    return (list_drift, list_counts, new_blocks)


def solution(mesh):
    placed = (
        P(("row", "col"), None),
        P(("row", "col"), None),
        P(("row", "col")),
        P(),
        P(),
        P(("row", "col")),
    )
    return jax.shard_map(
        local,
        mesh=mesh,
        in_specs=placed,
        out_specs=(P(("row", "col"), None), P(("row", "col")), P(("row", "col"))),
        check_vma=False,
    )
```

profile of v0, /device:TPU:0, one launch (start us, length us, event | category | flops | bytes accessed | tf_op | source)
XLA Modules:
  0.0 245.6 jit_solution(13785492173893013077)
XLA Ops:
  0.6 0.8 add_select_fusion
  2.0 0.7 compare_select_fusion
  2.7 4.5 %scatter_custom_fusion = s32[3072]{0:T(1024)S(1)} fusion(s32[1024]{0:T(1024)S(1)} %compare_select_fusion, s32[1024]{0:T(1024)} %param.10, s32[]{:T(128)} %constant.57.clone.1), kind=kCustom, calls=%fused_computation.32 | custom fusion | bytes 12800 | tf_op jit(solution)/shard_map/scatter | solution.py:66
  7.9 5.2 %all-to-all-start = ((s32[4,8,96]{2,1,0:T(8,128)}), s32[4,8,96]{2,1,0:T(8,128)S(1)}, u32[]{:S(2)}, u32[]{:S(2)}) async-start(s32[4,8,96]{2,1,0:T(8,128)} %reshape.51), calls=%async_computation | async-start | bytes 32768 | tf_op jit(solution)/shard_map/all_to_all | solution.py:78
  13.1 1.8 reshape.52
  14.8 1.2 copy.26
  16.0 0.9 reshape.53
  16.9 32.8 %while.10 = (s32[]{:T(128)}, f32[4,256,768]{2,1,0:T(8,128)}, s32[4,256,64]{1,0,2:T(4,128)}, bf16[256,64,12]{0,2,1:T(8,128)(2,1)}, s32[]{:T(128)}) while((s32[]{:T(128)}, f32[4,256,768]{2,1,0:T(8,128)}, s32[4,256,64]{1,0,2:T(4,128)}, bf16[256,64,12]{0,2,1:T(8,128)(2,1)}, s32[]{:T(128)}) %tuple.27), condition=%wide.region_3.4_spmd, body=%wide.region_2.3_spmd.sunk | while | flops 104857600 | bytes 6225997 | solution.py:22
  16.9 1.0 constant_dynamic-slice_fusion.2
  17.9 5.9 %fusion.27 = f32[256,64,12]{0,2,1:T(8,128)S(1)} fusion(bf16[256,64,12]{0,2,1:T(8,128)(2,1)} %get-tuple-element.90, s32[256,64]{0,1:T(8,128)S(1)} %bitcast.29), kind=kOutput, calls=%fused_computation.5.clone.1 | convolution fusion | flops 104857600 | bytes 1245184 | tf_op jit(solution)/shard_map/while/body/eval_jaxpr/bmk,kmj->bmj/dot_general | solution.py:19
  24.1 0.9 constant_dynamic-update-slice_fusion.2
  25.1 1.0 constant_dynamic-slice_fusion.2
  26.1 5.9 %fusion.27 = f32[256,64,12]{0,2,1:T(8,128)S(1)} fusion(bf16[256,64,12]{0,2,1:T(8,128)(2,1)} %get-tuple-element.90, s32[256,64]{0,1:T(8,128)S(1)} %bitcast.29), kind=kOutput, calls=%fused_computation.5.clone.1 | convolution fusion | flops 104857600 | bytes 1245184 | tf_op jit(solution)/shard_map/while/body/eval_jaxpr/bmk,kmj->bmj/dot_general | solution.py:19
  32.3 0.9 constant_dynamic-update-slice_fusion.2
  33.3 1.0 constant_dynamic-slice_fusion.2
  34.3 5.9 %fusion.27 = f32[256,64,12]{0,2,1:T(8,128)S(1)} fusion(bf16[256,64,12]{0,2,1:T(8,128)(2,1)} %get-tuple-element.90, s32[256,64]{0,1:T(8,128)S(1)} %bitcast.29), kind=kOutput, calls=%fused_computation.5.clone.1 | convolution fusion | flops 104857600 | bytes 1245184 | tf_op jit(solution)/shard_map/while/body/eval_jaxpr/bmk,kmj->bmj/dot_general | solution.py:19
  40.5 1.0 constant_dynamic-update-slice_fusion.2
  41.5 1.0 constant_dynamic-slice_fusion.2
  42.5 5.9 %fusion.27 = f32[256,64,12]{0,2,1:T(8,128)S(1)} fusion(bf16[256,64,12]{0,2,1:T(8,128)(2,1)} %get-tuple-element.90, s32[256,64]{0,1:T(8,128)S(1)} %bitcast.29), kind=kOutput, calls=%fused_computation.5.clone.1 | convolution fusion | flops 104857600 | bytes 1245184 | tf_op jit(solution)/shard_map/while/body/eval_jaxpr/bmk,kmj->bmj/dot_general | solution.py:19
  48.7 0.9 constant_dynamic-update-slice_fusion.2
  49.7 3.6 %fusion.4 = bf16[1024,768]{1,0:T(8,128)(2,1)S(1)} fusion(f32[4,256,768]{2,1,0:T(8,128)} %get-tuple-element.25, bf16[1024,768]{1,0:T(8,128)(2,1)S(1)} %copy-done, bf16[768,768]{1,0:T(8,128)(2,1)} %param.11), kind=kOutput, calls=%fused_computation.12 | convolution fusion | flops 1209532416 | bytes 7471104 | tf_op jit(solution)/shard_map/dot_general | solution.py:56
  53.3 8.2 %scatter_custom_fusion.1 = bf16[3072,768]{1,0:T(8,128)(2,1)} fusion(s32[1024]{0:T(1024)S(1)} %compare_select_fusion, bf16[1024,768]{1,0:T(8,128)(2,1)S(1)} %fusion.4, bf16[]{:T(256)} %constant.68.clone.1), kind=kCustom, calls=%fused_computation.17 | custom fusion | bytes 4718594 | tf_op jit(solution)/shard_map/scatter | solution.py:64
  61.5 4.9 %all-to-all-start.2 = ((bf16[4,8,96,768]{3,2,1,0:T(8,128)(2,1)}), bf16[4,8,96,768]{3,2,1,0:T(8,128)(2,1)}, u32[]{:S(2)}, u32[]{:S(2)}) async-start(bf16[4,8,96,768]{3,2,1,0:T(8,128)(2,1)} %bitcast.27), calls=%async_computation.2 | async-start | bytes 9437184 | tf_op jit(solution)/shard_map/all_to_all | solution.py:71
  67.1 52.4 %all-to-all-done.2 = bf16[4,8,96,768]{3,2,1,0:T(8,128)(2,1)} async-done(((bf16[4,8,96,768]{3,2,1,0:T(8,128)(2,1)}), bf16[4,8,96,768]{3,2,1,0:T(8,128)(2,1)}, u32[]{:S(2)}, u32[]{:S(2)}) %all-to-all-start.2) | async-done | bytes 4718624 | tf_op jit(solution)/shard_map/all_to_all | solution.py:71
  119.5 4.9 %all-to-all-start.1 = ((s32[4,8,96]{2,0,1:T(4,128)}), s32[4,8,96]{2,0,1:T(4,128)S(1)}, u32[]{:S(2)}, u32[]{:S(2)}) async-start(s32[4,8,96]{2,0,1:T(4,128)} %copy.24), calls=%async_computation.1 | async-start | bytes 32768 | tf_op jit(solution)/shard_map/all_to_all | solution.py:77
  124.4 4.9 %copy.29 = bf16[4,8,96,768]{3,2,0,1:T(8,128)(2,1)} copy(bf16[4,8,96,768]{3,2,1,0:T(8,128)(2,1)} %all-to-all-done.2) | data formatting | bytes 9437184 | tf_op jit(solution)/shard_map/all_to_all | solution.py:71
  129.3 0.8 all-to-all-done.1
  130.0 4.8 %all-to-all-start.3 = ((bf16[4,8,96,768]{3,2,0,1:T(8,128)(2,1)}), bf16[4,8,96,768]{3,2,0,1:T(8,128)(2,1)}, u32[]{:S(2)}, u32[]{:S(2)}) async-start(bf16[4,8,96,768]{3,2,0,1:T(8,128)(2,1)} %copy.29), calls=%async_computation.3 | async-start | bytes 9437184 | tf_op jit(solution)/shard_map/all_to_all | solution.py:70
  134.9 1.4 convert_reduce_fusion
  136.9 103.0 %all-to-all-done.3 = bf16[4,8,96,768]{3,2,0,1:T(8,128)(2,1)} async-done(((bf16[4,8,96,768]{3,2,0,1:T(8,128)(2,1)}), bf16[4,8,96,768]{3,2,0,1:T(8,128)(2,1)}, u32[]{:S(2)}, u32[]{:S(2)}) %all-to-all-start.3) | async-done | bytes 4718624 | tf_op jit(solution)/shard_map/all_to_all | solution.py:70
  239.9 2.7 %copy.30 = bf16[4,8,96,768]{3,2,1,0:T(8,128)(2,1)S(1)} copy(bf16[4,8,96,768]{3,2,0,1:T(8,128)(2,1)} %all-to-all-done.3) | data formatting | bytes 9437184 | tf_op jit(solution)/shard_map/all_to_all | solution.py:70
  242.6 3.0 %fusion.10 = f32[256,768]{1,0:T(8,128)} fusion(bf16[3072,768]{1,0:T(8,128)(2,1)S(1)} %bitcast.28, s32[3072]{0:T(1024)S(1)} %select_n.31, f32[256]{0:T(256)S(1)} %maximum_convert_fusion), kind=kOutput, calls=%fused_computation.20 | convolution fusion | flops 1208942592 | bytes 5518336 | tf_op jit(solution)/shard_map/dot_general | solution.py:29
  (28 shorter events, 3.9 us)
Async XLA Ops:
  0.6 49.1 %copy-start = (bf16[1024,768]{1,0:T(8,128)(2,1)S(1)}, bf16[1024,768]{1,0:T(8,128)(2,1)}, u32[]{:S(2)}) copy-start(bf16[1024,768]{1,0:T(8,128)(2,1)} %param.8) | copy-start | bytes 4718596
  7.9 53.7 %all-to-all-start = ((s32[4,8,96]{2,1,0:T(8,128)}), s32[4,8,96]{2,1,0:T(8,128)S(1)}, u32[]{:S(2)}, u32[]{:S(2)}) async-start(s32[4,8,96]{2,1,0:T(8,128)} %reshape.51), calls=%async_computation | async-start | bytes 32768 | tf_op jit(solution)/shard_map/all_to_all | solution.py:78
  61.5 58.0 %all-to-all-start.2 = ((bf16[4,8,96,768]{3,2,1,0:T(8,128)(2,1)}), bf16[4,8,96,768]{3,2,1,0:T(8,128)(2,1)}, u32[]{:S(2)}, u32[]{:S(2)}) async-start(bf16[4,8,96,768]{3,2,1,0:T(8,128)(2,1)} %bitcast.27), calls=%async_computation.2 | async-start | bytes 9437184 | tf_op jit(solution)/shard_map/all_to_all | solution.py:71
  119.5 10.5 %all-to-all-start.1 = ((s32[4,8,96]{2,0,1:T(4,128)}), s32[4,8,96]{2,0,1:T(4,128)S(1)}, u32[]{:S(2)}, u32[]{:S(2)}) async-start(s32[4,8,96]{2,0,1:T(4,128)} %copy.24), calls=%async_computation.1 | async-start | bytes 32768 | tf_op jit(solution)/shard_map/all_to_all | solution.py:77
  129.3 7.0 %copy-start.2 = (s32[256]{0:T(256)S(1)}, s32[256]{0:T(256)}, u32[]{:S(2)}) copy-start(s32[256]{0:T(256)} %param.13) | copy-start | bytes 3076
  130.0 109.8 %all-to-all-start.3 = ((bf16[4,8,96,768]{3,2,0,1:T(8,128)(2,1)}), bf16[4,8,96,768]{3,2,0,1:T(8,128)(2,1)}, u32[]{:S(2)}, u32[]{:S(2)}) async-start(bf16[4,8,96,768]{3,2,0,1:T(8,128)(2,1)} %copy.29), calls=%async_computation.3 | async-start | bytes 9437184 | tf_op jit(solution)/shard_map/all_to_all | solution.py:70
  136.9 105.7 %copy-start.1 = (s32[256]{0:T(256)}, s32[256]{0:T(256)S(1)}, u32[]{:S(2)}) copy-start(s32[256]{0:T(256)S(1)} %get-tuple-element.51) | copy-start | bytes 3076
where the time goes:
time: 247 us; the launch traced here: 246 us
  waiting for transfers between devices  156 us (63%)
  local copies, waits for them, and re-layouts  34.7 us (14%)
  matrix products  30.6 us (12%)
  starting transfers between devices  19.8 us (8%)
  other arithmetic  3.47 us (1%)
    all_to_all x1, waiting for transfers between devices, local(): lax.all_to_all(lax.all_to_all(send_rows, 'row', split_axis=0, concat_axis...  103 us
    all_to_all x1, waiting for transfers between devices, local(): lax.all_to_all(send_rows, 'row', split_axis=0, concat_axis=0, tiled=True)  52.4 us
    dot_general x4, matrix products, one_block(): jnp.einsum('bmk,kmj->bmj', picker, code_table, preferred_element_type=jnp...  23.5 us
    scatter x1, local copies, waits for them, and re-layouts, local(): send_rows = jnp.zeros((owner_total * slot_cap, feat_width), jnp.bfloat16)...  8.18 us
    all_to_all x1, starting transfers between devices, local(): lax.all_to_all(send_tags, 'row', split_axis=0, concat_axis=0, tiled=True)  5.19 us
  transfers between devices with their start and end apart: 4, of which 3 were waited for; matrix products, arithmetic and copies ran while one was open for 23% of the time, Pallas kernels for 0%

commit v1 on v0

--- a/solution.py
+++ b/solution.py
@@ -2,6 +2,18 @@
 import jax.numpy as jnp
 from jax import lax
 from jax.sharding import PartitionSpec as P
+
+
+def rotated_exchange(shard, axis, split, join):
+    ways, here = (lax.axis_size(axis), lax.axis_index(axis))
+    width = shard.shape[split] // ways
+    turned = jnp.roll(shard, -here * width, axis=split)
+    got = [lax.slice_in_dim(turned, 0, width, axis=split)]
+    for far in range(1, ways):
+        sent = lax.slice_in_dim(turned, far * width, (far + 1) * width, axis=split)
+        got.append(lax.ppermute(sent, axis, [(d, (d + far) % ways) for d in range(ways)]))
+    line = jnp.concatenate(got[::-1], axis=join)
+    return jnp.roll(line, (here + 1) * got[0].shape[join], axis=join)
 
 
 def decode_rows(codes, codebook):
@@ -68,11 +80,7 @@
     send_tags = send_tags.reshape(row_count, col_count, slot_cap)
     got_rows, got_tags = (
         lax.all_to_all(
-            lax.all_to_all(send_rows, "row", split_axis=0, concat_axis=0, tiled=True),
-            "col",
-            split_axis=1,
-            concat_axis=1,
-            tiled=True,
+            rotated_exchange(send_rows, "row", 0, 0), "col", split_axis=1, concat_axis=1, tiled=True
         ),
         lax.all_to_all(
             lax.all_to_all(send_tags, "row", split_axis=0, concat_axis=0, tiled=True),

time: 247 us -> 247 us (level)
  other arithmetic: 3.47 us -> 14.1 us
  waiting for transfers between devices: 156 us -> 147 us
    all_to_all x2 -> x1, waiting for transfers between devices: 155 us -> 103 us  [local(): lax.all_to_all(rotated_exchange(send_rows, 'row', 0, 0), 'col', split_axi...]
    all_to_all x1, waiting for transfers between devices: 0.01 us -> 43.2 us  [local(): lax.all_to_all(send_tags, 'row', split_axis=0, concat_axis=0, tiled=True)]
    concatenate x0 -> x2, other arithmetic: none -> 10.6 us  [the longest x1 6.61 us: rotated_exchange(): return jnp.roll(line, (here + 1) * got[0].shape[join], axis=join)]
    ppermute x0 -> x3, starting transfers between devices: none -> 5.06 us  [rotated_exchange(): lax.ppermute(sent, axis, [(d, (d + far) % ways) for d in range(ways)])]
    all_to_all x2 -> x1, local copies, waits for them, and re-layouts: 7.57 us -> 2.69 us  [local(): lax.all_to_all(rotated_exchange(send_rows, 'row', 0, 0), 'col', split_axi...]
    all_to_all x2 -> x1, starting transfers between devices: 9.72 us -> 5.22 us  [local(): lax.all_to_all(rotated_exchange(send_rows, 'row', 0, 0), 'col', split_axi...]
    dynamic_slice x0 -> x1, local copies, waits for them, and re-layouts: none -> 2.53 us  [rotated_exchange(): return jnp.roll(line, (here + 1) * got[0].shape[join], axis=join)]
  transfers between devices with their start and end apart: 4 -> 6, of which waited for: 3 -> 2; matrix products, arithmetic and copies ran while one was open for 23% -> 7% of each run, Pallas kernels for 0% -> 0%
where the time goes in v1:
time: 247 us; the launch traced here: 245 us
  waiting for transfers between devices  147 us (60%)
  local copies, waits for them, and re-layouts  34.2 us (14%)
  matrix products  30.6 us (12%)
  starting transfers between devices  18.8 us (8%)
  other arithmetic  14.1 us (6%)
    all_to_all x1, waiting for transfers between devices, local(): lax.all_to_all(rotated_exchange(send_rows, 'row', 0, 0), 'col', split_axi...  103 us
    all_to_all x1, waiting for transfers between devices, local(): lax.all_to_all(send_tags, 'row', split_axis=0, concat_axis=0, tiled=True)  43.2 us
    dot_general x4, matrix products, one_block(): jnp.einsum('bmk,kmj->bmj', picker, code_table, preferred_element_type=jnp...  23.5 us
    scatter x1, local copies, waits for them, and re-layouts, local(): send_rows = jnp.zeros((owner_total * slot_cap, feat_width), jnp.bfloat16)...  8.14 us
    concatenate x1, other arithmetic, rotated_exchange(): return jnp.roll(line, (here + 1) * got[0].shape[join], axis=join)  6.61 us
    all_to_all x1, starting transfers between devices, local(): lax.all_to_all(rotated_exchange(send_rows, 'row', 0, 0), 'col', split_axi...  5.22 us
    ppermute x3, starting transfers between devices, rotated_exchange(): lax.ppermute(sent, axis, [(d, (d + far) % ways) for d in range(ways)])  5.06 us
  transfers between devices with their start and end apart: 6, of which 2 were waited for; matrix products, arithmetic and copies ran while one was open for 7% of the time, Pallas kernels for 0%

profile of v1, /device:TPU:0, one launch (start us, length us, event | category | flops | bytes accessed | tf_op | source)
XLA Modules:
  0.0 245.1 jit_solution(14824163437519412516)
XLA Ops:
  2.7 1.2 copy.26
  3.9 0.9 reshape.53
  4.8 1.8 reshape.52
  6.5 32.8 %while.10 = (s32[]{:T(128)}, f32[4,256,768]{2,1,0:T(8,128)}, s32[4,256,64]{1,0,2:T(4,128)}, bf16[256,64,12]{0,2,1:T(8,128)(2,1)}, s32[]{:T(128)}) while((s32[]{:T(128)}, f32[4,256,768]{2,1,0:T(8,128)}, s32[4,256,64]{1,0,2:T(4,128)}, bf16[256,64,12]{0,2,1:T(8,128)(2,1)}, s32[]{:T(128)}) %tuple.31), condition=%wide.region_3.4_spmd, body=%wide.region_2.3_spmd.sunk | while | flops 104857600 | bytes 6226497 | solution.py:34
  6.5 1.0 constant_dynamic-slice_fusion.2
  7.6 5.9 %fusion.36 = f32[256,64,12]{0,2,1:T(8,128)S(1)} fusion(bf16[256,64,12]{0,2,1:T(8,128)(2,1)} %get-tuple-element.95, s32[256,64]{0,1:T(8,128)S(1)} %bitcast.29), kind=kOutput, calls=%fused_computation.5.clone.1 | convolution fusion | flops 104857600 | bytes 1245184 | tf_op jit(solution)/shard_map/while/body/eval_jaxpr/bmk,kmj->bmj/dot_general | solution.py:31
  13.8 1.0 constant_dynamic-update-slice_fusion.2
  14.8 1.0 constant_dynamic-slice_fusion.2
  15.8 5.9 %fusion.36 = f32[256,64,12]{0,2,1:T(8,128)S(1)} fusion(bf16[256,64,12]{0,2,1:T(8,128)(2,1)} %get-tuple-element.95, s32[256,64]{0,1:T(8,128)S(1)} %bitcast.29), kind=kOutput, calls=%fused_computation.5.clone.1 | convolution fusion | flops 104857600 | bytes 1245184 | tf_op jit(solution)/shard_map/while/body/eval_jaxpr/bmk,kmj->bmj/dot_general | solution.py:31
  22.0 1.0 constant_dynamic-update-slice_fusion.2
  23.0 1.0 constant_dynamic-slice_fusion.2
  24.0 5.9 %fusion.36 = f32[256,64,12]{0,2,1:T(8,128)S(1)} fusion(bf16[256,64,12]{0,2,1:T(8,128)(2,1)} %get-tuple-element.95, s32[256,64]{0,1:T(8,128)S(1)} %bitcast.29), kind=kOutput, calls=%fused_computation.5.clone.1 | convolution fusion | flops 104857600 | bytes 1245184 | tf_op jit(solution)/shard_map/while/body/eval_jaxpr/bmk,kmj->bmj/dot_general | solution.py:31
  30.2 1.0 constant_dynamic-update-slice_fusion.2
  31.2 1.0 constant_dynamic-slice_fusion.2
  32.2 5.9 %fusion.36 = f32[256,64,12]{0,2,1:T(8,128)S(1)} fusion(bf16[256,64,12]{0,2,1:T(8,128)(2,1)} %get-tuple-element.95, s32[256,64]{0,1:T(8,128)S(1)} %bitcast.29), kind=kOutput, calls=%fused_computation.5.clone.1 | convolution fusion | flops 104857600 | bytes 1245184 | tf_op jit(solution)/shard_map/while/body/eval_jaxpr/bmk,kmj->bmj/dot_general | solution.py:31
  38.4 0.9 constant_dynamic-update-slice_fusion.2
  39.4 3.6 %fusion.12 = bf16[1024,768]{1,0:T(8,128)(2,1)S(1)} fusion(f32[4,256,768]{2,1,0:T(8,128)} %get-tuple-element.26, bf16[1024,768]{1,0:T(8,128)(2,1)S(1)} %copy-done, bf16[768,768]{1,0:T(8,128)(2,1)} %param.13), kind=kOutput, calls=%fused_computation.30 | convolution fusion | flops 1209532416 | bytes 7471104 | tf_op jit(solution)/shard_map/dot_general | solution.py:68
  43.0 8.1 %scatter_custom_fusion.1 = bf16[3072,768]{1,0:T(8,128)(2,1)} fusion(s32[1024]{0:T(1024)S(1)} %compare_select_fusion, bf16[1024,768]{1,0:T(8,128)(2,1)S(1)} %fusion.12, bf16[]{:T(256)} %constant.86.clone.1), kind=kCustom, calls=%fused_computation.35 | custom fusion | bytes 4718594 | tf_op jit(solution)/shard_map/scatter | solution.py:76
  51.2 4.0 %fusion.10 = bf16[4,8,96,768]{3,2,1,0:T(8,128)(2,1)S(1)} fusion(s32[]{:T(128)S(6)} %select_n.47, bf16[4,8,96,768]{3,2,1,0:T(8,128)(2,1)} %bitcast.27), kind=kLoop, calls=%fused_computation.26 | loop fusion | flops 2359296 | bytes 9437188 | tf_op jit(solution)/shard_map/jit(_roll_dynamic)/concatenate | solution.py:10
  55.2 1.9 fusion.28
  57.0 3.9 %collective-permute-start = (bf16[1,8,96,768]{3,2,1,0:T(8,128)(2,1)}, bf16[1,8,96,768]{3,2,1,0:T(8,128)(2,1)}, u32[]{:S(2)}, u32[]{:S(2)}) collective-permute-start(bf16[1,8,96,768]{3,2,1,0:T(8,128)(2,1)} %get-tuple-element.56), channel_id=1, source_target_pairs={{0,24},{8,0},{16,8},{24,16},{1,25},{9,1},{17,9},{25,17},{2,26},{10... | collective-permute-start | bytes 3538952 | tf_op jit(solution)/shard_map/ppermute | solution.py:14
  62.1 4.5 %scatter_custom_fusion = s32[3072]{0:T(1024)S(1)} fusion(s32[1024]{0:T(1024)S(1)} %compare_select_fusion, s32[1024]{0:T(1024)} %param.12, s32[]{:T(128)} %constant.75.clone.1), kind=kCustom, calls=%fused_computation.50 | custom fusion | bytes 12800 | tf_op jit(solution)/shard_map/scatter | solution.py:78
  67.3 3.6 %all-to-all-start = ((s32[4,8,96]{2,1,0:T(8,128)}), s32[4,8,96]{2,1,0:T(8,128)S(1)}, u32[]{:S(2)}, u32[]{:S(2)}) async-start(s32[4,8,96]{2,1,0:T(8,128)} %reshape.51), calls=%async_computation | async-start | bytes 32768 | tf_op jit(solution)/shard_map/all_to_all | solution.py:86
  70.9 43.2 %all-to-all-done = s32[4,8,96]{2,1,0:T(8,128)S(1)} async-done(((s32[4,8,96]{2,1,0:T(8,128)}), s32[4,8,96]{2,1,0:T(8,128)S(1)}, u32[]{:S(2)}, u32[]{:S(2)}) %all-to-all-start) | async-done | bytes 12320 | tf_op jit(solution)/shard_map/all_to_all | solution.py:86
  114.8 4.9 %all-to-all-start.1 = ((s32[4,8,96]{2,0,1:T(4,128)}), s32[4,8,96]{2,0,1:T(4,128)S(1)}, u32[]{:S(2)}, u32[]{:S(2)}) async-start(s32[4,8,96]{2,0,1:T(4,128)} %copy.24), calls=%async_computation.1 | async-start | bytes 32768 | tf_op jit(solution)/shard_map/all_to_all | solution.py:85
  119.7 6.6 %fusion.6 = bf16[4,8,96,768]{3,2,1,0:T(8,128)(2,1)S(1)} fusion(s32[]{:T(128)S(6)} %select_n.49, bf16[1,8,96,768]{3,2,1,0:T(8,128)(2,1)} %collective-permute-done, bf16[1,8,96,768]{3,2,1,0:T(8,128)(2,1)} %collective-permute-done.1, bf16[1,8,96,768]{3,2,1,0:T(8,128)(2,1)} %collective-permute-done.2, bf16[1,8,96,768]{3,2,1,0:T(8,128)(2,1)S(1)} %get-tuple-element.53), kind=kLoop, calls=%fused_computation.22 | loop fusion | flops 16515072 | bytes 9437188 | tf_op jit(solution)/shard_map/jit(_roll_dynamic)/concatenate | solution.py:16
  126.3 2.5 %copy.29 = bf16[4,8,96,768]{3,2,0,1:T(8,128)(2,1)} copy(bf16[4,8,96,768]{3,2,1,0:T(8,128)(2,1)S(1)} %fusion.6) | data formatting | bytes 9437184 | tf_op jit(solution)/shard_map/jit(_roll_dynamic)/dynamic_slice | solution.py:16
  128.8 5.2 %all-to-all-start.2 = ((bf16[4,8,96,768]{3,2,0,1:T(8,128)(2,1)}), bf16[4,8,96,768]{3,2,0,1:T(8,128)(2,1)}, u32[]{:S(2)}, u32[]{:S(2)}) async-start(bf16[4,8,96,768]{3,2,0,1:T(8,128)(2,1)} %copy.29), calls=%async_computation.2 | async-start | bytes 9437184 | tf_op jit(solution)/shard_map/all_to_all | solution.py:82
  134.1 1.4 convert_reduce_fusion
  136.1 103.3 %all-to-all-done.2 = bf16[4,8,96,768]{3,2,0,1:T(8,128)(2,1)} async-done(((bf16[4,8,96,768]{3,2,0,1:T(8,128)(2,1)}), bf16[4,8,96,768]{3,2,0,1:T(8,128)(2,1)}, u32[]{:S(2)}, u32[]{:S(2)}) %all-to-all-start.2) | async-done | bytes 4718624 | tf_op jit(solution)/shard_map/all_to_all | solution.py:82
  239.4 2.7 %copy.30 = bf16[4,8,96,768]{3,2,1,0:T(8,128)(2,1)S(1)} copy(bf16[4,8,96,768]{3,2,0,1:T(8,128)(2,1)} %all-to-all-done.2) | data formatting | bytes 9437184 | tf_op jit(solution)/shard_map/all_to_all | solution.py:82
  242.1 3.0 %fusion.18 = f32[256,768]{1,0:T(8,128)} fusion(bf16[3072,768]{1,0:T(8,128)(2,1)S(1)} %bitcast.28, s32[3072]{0:T(1024)S(1)} %select_n.41, f32[256]{0:T(256)S(1)} %maximum_convert_fusion), kind=kOutput, calls=%fused_computation.38 | convolution fusion | flops 1208942592 | bytes 5518336 | tf_op jit(solution)/shard_map/dot_general | solution.py:41
  (35 shorter events, 6.6 us)
Async XLA Ops:
  0.6 38.7 %copy-start = (bf16[1024,768]{1,0:T(8,128)(2,1)S(1)}, bf16[1024,768]{1,0:T(8,128)(2,1)}, u32[]{:S(2)}) copy-start(bf16[1024,768]{1,0:T(8,128)(2,1)} %param.10) | copy-start | bytes 4718596
  57.0 62.6 %collective-permute-start = (bf16[1,8,96,768]{3,2,1,0:T(8,128)(2,1)}, bf16[1,8,96,768]{3,2,1,0:T(8,128)(2,1)}, u32[]{:S(2)}, u32[]{:S(2)}) collective-permute-start(bf16[1,8,96,768]{3,2,1,0:T(8,128)(2,1)} %get-tuple-element.56), channel_id=1, source_target_pairs={{0,24},{8,0},{16,8},{24,16},{1,25},{9,1},{17,9},{25,17},{2,26},{10... | collective-permute-start | bytes 3538952 | tf_op jit(solution)/shard_map/ppermute | solution.py:14
  61.0 58.6 %collective-permute-start.1 = (bf16[1,8,96,768]{3,2,1,0:T(8,128)(2,1)}, bf16[1,8,96,768]{3,2,1,0:T(8,128)(2,1)}, u32[]{:S(2)}, u32[]{:S(2)}) collective-permute-start(bf16[1,8,96,768]{3,2,1,0:T(8,128)(2,1)} %get-tuple-element.55), channel_id=1, source_target_pairs={{0,16},{8,24},{16,0},{24,8},{1,17},{9,25},{17,1},{25,9},{2,18},{10... | collective-permute-start | bytes 3538952 | tf_op jit(solution)/shard_map/ppermute | solution.py:14
  61.5 58.2 %collective-permute-start.2 = (bf16[1,8,96,768]{3,2,1,0:T(8,128)(2,1)}, bf16[1,8,96,768]{3,2,1,0:T(8,128)(2,1)}, u32[]{:S(2)}, u32[]{:S(2)}) collective-permute-start(bf16[1,8,96,768]{3,2,1,0:T(8,128)(2,1)} %get-tuple-element.54), channel_id=1, source_target_pairs={{0,8},{8,16},{16,24},{24,0},{1,9},{9,17},{17,25},{25,1},{2,10},{10... | collective-permute-start | bytes 3538952 | tf_op jit(solution)/shard_map/ppermute | solution.py:14
  67.3 46.9 %all-to-all-start = ((s32[4,8,96]{2,1,0:T(8,128)}), s32[4,8,96]{2,1,0:T(8,128)S(1)}, u32[]{:S(2)}, u32[]{:S(2)}) async-start(s32[4,8,96]{2,1,0:T(8,128)} %reshape.51), calls=%async_computation | async-start | bytes 32768 | tf_op jit(solution)/shard_map/all_to_all | solution.py:86
  114.8 14.1 %all-to-all-start.1 = ((s32[4,8,96]{2,0,1:T(4,128)}), s32[4,8,96]{2,0,1:T(4,128)S(1)}, u32[]{:S(2)}, u32[]{:S(2)}) async-start(s32[4,8,96]{2,0,1:T(4,128)} %copy.24), calls=%async_computation.1 | async-start | bytes 32768 | tf_op jit(solution)/shard_map/all_to_all | solution.py:85
  128.8 6.7 %copy-start.2 = (s32[256]{0:T(256)S(1)}, s32[256]{0:T(256)}, u32[]{:S(2)}) copy-start(s32[256]{0:T(256)} %param.15) | copy-start | bytes 3076
  128.8 110.5 %all-to-all-start.2 = ((bf16[4,8,96,768]{3,2,0,1:T(8,128)(2,1)}), bf16[4,8,96,768]{3,2,0,1:T(8,128)(2,1)}, u32[]{:S(2)}, u32[]{:S(2)}) async-start(bf16[4,8,96,768]{3,2,0,1:T(8,128)(2,1)} %copy.29), calls=%async_computation.2 | async-start | bytes 9437184 | tf_op jit(solution)/shard_map/all_to_all | solution.py:82
  136.1 106.0 %copy-start.1 = (s32[256]{0:T(256)}, s32[256]{0:T(256)S(1)}, u32[]{:S(2)}) copy-start(s32[256]{0:T(256)S(1)} %get-tuple-element.52) | copy-start | bytes 3076
